TPU v7x, 32 devices: a whole 2x2x4 slice. The times are simulated.
32 devices in a mesh: groups: 2 (over y), ep: 4 (over z), tp: 2 (over x), dp: 2 (over core).
Axes of the slice: x: 2, y: 2, z: 4, core: 2. Of those that a mesh axis runs over, the one named last changes fastest.
Arguments:
- tokens: bfloat16 [256, 5120], P(('groups', 'ep', 'tp', 'dp')), parts along dimension 0, may hold values from -6 to 6
- route_weights: float32 [256, 8], P(('groups', 'ep', 'tp', 'dp')), parts along dimension 0, may hold values from 0.1 to 1
- expert_ids: int32 [256, 8], P(('groups', 'ep', 'tp', 'dp')), parts along dimension 0, may hold values from 0 to 31, all different within a row; in each aligned block of 8 rows (0 to 7, 8 to 15, ...) at most 4 rows name the same one
- gate_weight: bfloat16 [32, 5120, 1024], P('ep', None, ('tp', 'dp')), may hold values from -0.078125 to 0.078125
- up_weight: bfloat16 [32, 5120, 1024], P('ep', None, ('tp', 'dp')), may hold values from -0.078125 to 0.078125
- down_weight: bfloat16 [32, 1024, 5120], P('ep', None, ('tp', 'dp')), may hold values from -0.1875 to 0.1875
Outputs:
- combined: bfloat16 [256, 5120], P(('groups', 'ep', 'tp', 'dp')), parts along dimension 0
There are 2 independent parts, one for each index of `groups`. A program takes and returns all parts, laid end to end along the dimension named above; an argument that names none is the same for every part. Nothing has to cross between parts.
Inputs may be any that keep to these rules, and one draw needn't show every extreme that they name: `expert_ids`: each row names 8 different experts. Among the 8 rows of one device no expert is named more than 4 times, and in every draw some device's rows name some expert exactly 4 times.
All inputs are finite; a program needn't handle non-finite values.
Results may differ from a plain program's by a relative error of at most 0.0057.
Values may be sent and summed in bfloat16 or wider, within the bound.
A program may use at most 128 MiB of HBM per device.

v0:
```python
import jax
import jax.numpy as jnp
from jax import lax
from jax.sharding import PartitionSpec as P

CAP = 4


def route_table(ids, experts, capacity):
    tok_count, top_count = ids.shape
    flat = ids.reshape(-1)
    onehot = (flat[:, None] == jnp.arange(experts, dtype=jnp.int32)[None, :]).astype(jnp.int32)
    slots = jnp.sum(onehot * jnp.cumsum(onehot, axis=0), axis=1) - 1
    place = flat * capacity + slots
    owner = jnp.arange(tok_count * top_count, dtype=jnp.int32) // top_count
    table = jnp.full((experts * capacity,), tok_count, jnp.int32).at[place].set(owner)
    return (place, table)


def per_device(tokens, route_weights, expert_ids, gate_weight, up_weight, down_weight):
    n_owner = lax.axis_size("ep")
    tok_count, top_count = expert_ids.shape
    exp_local = gate_weight.shape[0]
    experts = exp_local * n_owner
    width = tokens.shape[1]
    place, table = route_table(expert_ids, experts, CAP)
    sendbuf = jnp.take(tokens, table, axis=0, mode="fill", fill_value=0).reshape(
        experts, CAP, width
    )
    arrived = lax.all_to_all(sendbuf, "ep", split_axis=0, concat_axis=0, tiled=True)
    arrived = arrived.reshape(1, n_owner, exp_local, CAP, width)
    piece = lax.all_gather(arrived, ("tp", "dp"), axis=0, tiled=True)
    gate = jnp.einsum("gsecd,edf->gsecf", piece, gate_weight, preferred_element_type=jnp.float32)
    up = jnp.einsum("gsecd,edf->gsecf", piece, up_weight, preferred_element_type=jnp.float32)
    hidden = (jax.nn.silu(gate) * up).astype(jnp.bfloat16)
    partial_out = jnp.einsum(
        "gsecf,efd->gsecd",
        lax.all_gather(hidden, ("tp", "dp"), axis=4, tiled=True),
        down_weight,
        preferred_element_type=jnp.float32,
    )
    expert_out = partial_out.astype(jnp.bfloat16)
    mine = lax.all_to_all(expert_out, ("tp", "dp"), split_axis=0, concat_axis=4, tiled=True)
    mine = mine.reshape(n_owner * exp_local, CAP, width)
    returned = lax.all_to_all(mine, "ep", split_axis=0, concat_axis=0, tiled=True)
    picked = jnp.take(returned.reshape(experts * CAP, width), place, axis=0)
    picked = picked.reshape(tok_count, top_count, width).astype(jnp.float32)
    combined = jnp.sum(picked * route_weights[:, :, None], axis=1)
    return combined.astype(jnp.bfloat16)


def solution(mesh):
    return jax.shard_map(
        per_device,
        mesh=mesh,
        in_specs=(
            P(("groups", "ep", "tp", "dp"), None),
            P(("groups", "ep", "tp", "dp"), None),
            P(("groups", "ep", "tp", "dp"), None),
            P("ep", None, ("tp", "dp")),
            P("ep", None, ("tp", "dp")),
            P("ep", None, ("tp", "dp")),
        ),
        out_specs=P(("groups", "ep", "tp", "dp"), None),
        check_vma=False,
    )
```

profile of v0, /device:TPU:0, one launch (start us, length us, event | category | flops | bytes accessed | tf_op | source)
XLA Modules:
  0.0 212.0 jit_solution(12040743795864728024)
XLA Ops:
  6.5 0.0 copy-start
  6.5 0.0 all-gather.3.cloned.1.call-start
  6.5 0.8 reshape.76
  7.3 0.7 broadcast_multiply_fusion
  8.0 0.1 fusion.24
  8.1 0.1 reduce_window_sum.11
  8.2 0.2 select_reduce_fusion
  8.4 0.1 mul.40
  8.5 0.8 scatter_custom_fusion
  9.3 0.0 copy-done
  9.3 1.3 gather_fusion
  10.6 0.5 gather.13
  11.1 0.1 broadcast_in_dim.32
  11.3 0.7 broadcast_select_fusion
  11.9 37.5 %all_to_all.25 = bf16[32,4,5120]{2,1,0:T(4,128)(2,1)S(1)} all-to-all(bf16[32,4,5120]{2,1,0:T(4,128)(2,1)S(1)} %broadcast_select_fusion), channel_id=1, replica_groups=mesh['groups'=2,'ep'=4,'tp'=2,'dp'=2] {'ep'}, dimensions={0} | all-to-all | bytes 2621440 | tf_op jit(solution)/shard_map/all_to_all | solution.py:30
  49.4 1.7 copy.13
  51.1 0.0 all-gather.3.cloned.1.call-update
  51.1 0.2 all-gather.5.cloned.1.call-start
  51.3 39.5 %all-gather.3.cloned.1.call-done = bf16[4,4,8,4,5120]{4,3,1,0,2:T(4,128)(2,1)} async-done(((bf16[1,4,8,4,5120]{4,3,1,0,2:T(4,128)(2,1)}), bf16[4,4,8,4,5120]{4,3,1,0,2:T(4,128)(2,1)}) %all-gather.3.cloned.1.call-update) | async-done | bytes 5242896 | tf_op jit(solution)/shard_map/all_gather | solution.py:32
  90.8 0.0 copy-start.4
  90.8 13.1 %fusion.12 = f32[4,4,8,4,256]{4,3,1,0,2:T(4,128)S(1)} fusion(bf16[4,4,8,4,5120]{4,3,1,0,2:T(4,128)(2,1)} %all-gather.3.cloned.1.call-done, bf16[8,5120,256]{2,1,0:T(8,128)(2,1)} %param.9), kind=kOutput, calls=%fused_computation.13 | convolution fusion | flops 1342177280 | bytes 26738688 | tf_op jit(solution)/shard_map/gsecd,edf->gsecf/dot_general | solution.py:33
  103.9 0.0 copy-done.4
  103.9 12.2 %fusion.21 = bf16[4,4,8,4,256]{4,3,1,0,2:T(4,128)(2,1)} fusion(bf16[4,4,8,4,5120]{4,3,1,0,2:T(4,128)(2,1)S(1)} %copy-done.4, bf16[8,5120,256]{2,1,0:T(8,128)(2,1)} %param.10, f32[4,4,8,4,256]{4,3,1,0,2:T(4,128)S(1)} %fusion.12), kind=kOutput, calls=%fused_computation.16 | convolution fusion | flops 1342963712 | bytes 27000832 | tf_op jit(solution)/shard_map/gsecd,edf->gsecf/dot_general | solution.py:34
  116.1 0.0 all-gather.5.cloned.1.call-update
  116.1 17.0 %all-gather.5.cloned.1.call-done = bf16[4,4,8,4,1024]{4,3,1,0,2:T(4,128)(2,1)} async-done(((bf16[4,4,8,4,256]{4,3,1,0,2:T(4,128)(2,1)}), bf16[4,4,8,4,1024]{4,3,1,0,2:T(4,128)(2,1)}) %all-gather.5.cloned.1.call-update) | async-done | bytes 1048592 | tf_op jit(solution)/shard_map/all_gather | solution.py:38
  133.1 11.3 %fusion.9 = bf16[4,4,8,4,1280]{4,3,1,0,2:T(4,128)(2,1)S(1)} fusion(bf16[4,4,8,4,1024]{4,3,1,0,2:T(4,128)(2,1)} %all-gather.5.cloned.1.call-done, bf16[8,1024,1280]{2,1,0:T(8,128)(2,1)} %param.11), kind=kOutput, calls=%fused_computation.10 | convolution fusion | flops 1342832640 | bytes 23330816 | tf_op jit(solution)/shard_map/gsecf,efd->gsecd/dot_general | solution.py:36
  144.4 0.5 copy.14
  144.9 19.7 %all_to_all.26 = bf16[4,4,8,4,1280]{4,3,1,2,0:T(4,128)(2,1)S(1)} all-to-all(bf16[4,4,8,4,1280]{4,3,1,2,0:T(4,128)(2,1)S(1)} %copy.14), channel_id=1, replica_groups=mesh['groups'=2,'ep'=4,'tp'=2,'dp'=2] {'tp','dp'}, dimensions={0} | all-to-all | bytes 2621440 | tf_op jit(solution)/shard_map/all_to_all | solution.py:43
  164.6 1.0 copy.22
  165.6 1.4 reshape.108
  167.0 0.0 copy-start.2
  167.0 4.7 %all-to-all-start.2 = ((bf16[32,4,5120]{2,1,0:T(4,128)(2,1)}), bf16[32,4,5120]{2,1,0:T(4,128)(2,1)S(1)}, u32[]{:S(2)}, u32[]{:S(2)}) async-start(bf16[32,4,5120]{2,1,0:T(4,128)(2,1)} %reshape.108), calls=%async_computation.2 | async-start | bytes 2621440 | tf_op jit(solution)/shard_map/all_to_all | solution.py:45
  171.7 0.1 sub.15
  171.8 0.0 copy-done.2
  171.8 30.9 %all-to-all-done.2 = bf16[32,4,5120]{2,1,0:T(4,128)(2,1)S(1)} async-done(((bf16[32,4,5120]{2,1,0:T(4,128)(2,1)}), bf16[32,4,5120]{2,1,0:T(4,128)(2,1)S(1)}, u32[]{:S(2)}, u32[]{:S(2)}) %all-to-all-start.2) | async-done | bytes 1310752 | tf_op jit(solution)/shard_map/all_to_all | solution.py:45
  202.7 0.3 reshape.79
  203.0 0.0 copy-start.3
  203.0 0.0 copy-start.1
  203.0 0.9 gather_fusion.1
  204.0 0.0 copy-done.3
  204.0 1.2 multiply_reduce_fusion
  205.1 0.0 copy-done.1
  (8 shorter events, 0.0 us)
Async XLA Ops:
  6.5 2.8 %copy-start = (bf16[8,5120]{1,0:T(8,128)(2,1)S(1)}, bf16[8,5120]{1,0:T(8,128)(2,1)}, u32[]{:S(2)}) copy-start(bf16[8,5120]{1,0:T(8,128)(2,1)} %param.6) | copy-start | bytes 245764
  6.5 84.3 %all-gather.3.cloned.1.call-start = ((), (), s32[]{:S(2)}) async-start(), calls=%async_computation.3 | async-start | bytes 6553600 | tf_op jit(solution)/shard_map/all_gather | solution.py:32
  51.1 82.0 %all-gather.5.cloned.1.call-start = ((), (), s32[]{:S(2)}) async-start(), calls=%async_computation.4 | async-start | bytes 1310720 | tf_op jit(solution)/shard_map/all_gather | solution.py:38
  90.8 13.1 %copy-start.4 = (bf16[4,4,8,4,5120]{4,3,1,0,2:T(4,128)(2,1)S(1)}, bf16[4,4,8,4,5120]{4,3,1,0,2:T(4,128)(2,1)}, u32[]{:S(2)}) copy-start(bf16[4,4,8,4,5120]{4,3,1,0,2:T(4,128)(2,1)} %all-gather.3.cloned.1.call-done) | copy-start | bytes 15728644
  167.0 4.8 %copy-start.2 = (s32[8,8]{1,0:T(8,128)S(1)}, s32[8,8]{1,0:T(8,128)}, u32[]{:S(2)}) copy-start(s32[8,8]{1,0:T(8,128)} %param.8) | copy-start | bytes 772
  167.0 35.7 %all-to-all-start.2 = ((bf16[32,4,5120]{2,1,0:T(4,128)(2,1)}), bf16[32,4,5120]{2,1,0:T(4,128)(2,1)S(1)}, u32[]{:S(2)}, u32[]{:S(2)}) async-start(bf16[32,4,5120]{2,1,0:T(4,128)(2,1)} %reshape.108), calls=%async_computation.2 | async-start | bytes 2621440 | tf_op jit(solution)/shard_map/all_to_all | solution.py:45
  203.0 1.0 copy-start.3
  203.0 2.1 %copy-start.1 = (bf16[8,5120]{1,0:T(8,128)(2,1)S(1)}, bf16[8,5120]{1,0:T(8,128)(2,1)}, u32[]{:S(2)}) copy-start(bf16[8,5120]{1,0:T(8,128)(2,1)} %param.6) | copy-start | bytes 245764
Sparse Core Ops, SparseCore 0:
  51.2 39.5 all-gather.2
  116.2 16.8 all-gather.4
where the time goes:
time: 212 us
  waiting for transfers between devices  87.3 us (41%)
  blocking collectives  57.2 us (27%)
  matrix products  36.6 us (17%)
  between operations  13.6 us (6%)
  local copies, waits for them, and re-layouts  9.45 us (4%)
  starting transfers between devices  4.95 us (2%)
  other arithmetic  2.91 us (1%)
    all_gather x1, waiting for transfers between devices, per_device(): piece = lax.all_gather(arrived, ('tp', 'dp'), axis=0, tiled=True)  39.5 us
    all_to_all x1, blocking collectives, per_device(): lax.all_to_all(sendbuf, 'ep', split_axis=0, concat_axis=0, tiled=True)  37.5 us
    all_to_all x1, waiting for transfers between devices, per_device(): lax.all_to_all(mine, 'ep', split_axis=0, concat_axis=0, tiled=True)  30.9 us
    all_to_all x1, blocking collectives, per_device(): lax.all_to_all(expert_out, ('tp', 'dp'), split_axis=0, concat_axis=4, til...  19.7 us
    all_gather x1, waiting for transfers between devices, per_device(): lax.all_gather(hidden, ('tp', 'dp'), axis=4, tiled=True)  17 us
    dot_general x1, matrix products, per_device(): jnp.einsum('gsecd,edf->gsecf', piece, gate_weight, preferred_element_type...  13.1 us
    dot_general x1, matrix products, per_device(): jnp.einsum('gsecd,edf->gsecf', piece, up_weight, preferred_element_type=j...  12.2 us
    dot_general x1, matrix products, per_device(): jnp.einsum('gsecf,efd->gsecd', lax.all_gather(hidden, ('tp', 'dp'), axis=...  11.3 us
  transfers between devices with their start and end apart: 3, of which 3 were waited for; matrix products, arithmetic and copies ran while one was open for 0% of the time, Pallas kernels for 0%

commit v1 on v0

v1 whole, which is shorter than its diff:
```python
import functools

import jax
import jax.numpy as jnp
from jax import lax
from jax.experimental import pallas as pl
from jax.experimental.pallas import tpu as pltpu
from jax.sharding import PartitionSpec as P

MESH = pl.DeviceIdType.MESH
LANES = 128
CHUNKS = 2
SLOTS = 12


def routed_rows(tokens, route_weights, expert_ids, experts, chunks, ext):
    lane = jnp.arange(experts, dtype=jnp.int32)
    dense = jnp.sum(
        jnp.where(expert_ids[:, :, None] == lane, route_weights[:, :, None], 0.0), axis=1
    )
    first = lax.reduce_precision(dense, 8, 7)
    second = lax.reduce_precision(dense - first, 8, 7)
    third = dense - first - second
    side = jnp.concatenate([first, second, third], axis=1).astype(jnp.bfloat16)
    side = jnp.pad(side, ((0, 0), (0, ext - side.shape[1])))
    rows, width = tokens.shape
    depth = width // chunks
    return jnp.stack(
        [
            jnp.concatenate([tokens[:, k * depth : (k + 1) * depth], side], axis=1)
            for k in range(chunks)
        ]
    )


def kernel(
    dims,
    xin,
    gate_hbm,
    up_hbm,
    down_hbm,
    out,
    xr,
    x2,
    gbuf,
    ubuf,
    dbuf,
    acc,
    hid,
    pbuf,
    back,
    g_sem,
    u_sem,
    d_sem,
    own_sem,
    xs_sem,
    xr_sem,
    hs_sem,
    hr_sem,
    ps_sem,
    pr_sem,
):
    n_ep, n_tp, n_dp, experts = dims
    nq = n_tp * n_dp
    nb = n_ep * nq
    chunks, _, rows, _ = xr.shape
    _, count, depth = x2.shape
    slots = gbuf.shape[0]
    local = acc.shape[0]
    ff = gbuf.shape[2]
    tiles, _, full, tile = dbuf.shape
    units = chunks * local
    mt = min(count, 128)
    mb = mt // rows
    msteps = count // mt

    z, x, c = lax.axis_index("ep"), lax.axis_index("tp"), lax.axis_index("dp")
    q = x * n_dp + c
    me = z * nq + q

    def weights_in(u):
        k, e = u // local, u % local
        s = u % slots
        span = pl.ds(pl.multiple_of(k * depth, depth), depth)
        return (
            pltpu.make_async_copy(gate_hbm.at[e, span, :], gbuf.at[s], g_sem.at[s]),
            pltpu.make_async_copy(up_hbm.at[e, span, :], ubuf.at[s], u_sem.at[s]),
        )

    def down_in(j):
        return pltpu.make_async_copy(
            down_hbm.at[:, :, j * tile : (j + 1) * tile], dbuf.at[j], d_sem.at[j]
        )

    for u in range(min(slots, units)):
        for copy in weights_in(u):
            copy.start()
    if units <= slots:
        for j in range(tiles):
            down_in(j).start()
    own = pltpu.make_async_copy(xin, xr.at[:, me], own_sem)
    own.start()

    barrier = pltpu.get_barrier_semaphore()

    def others(act):
        for dz in range(n_ep):
            for dx in range(n_tp):
                for dc in range(n_dp):
                    if dz or dx or dc:
                        act(lax.rem(z + dz, n_ep), lax.rem(x + dx, n_tp), lax.rem(c + dc, n_dp))

    others(
        lambda a, b, d: pl.semaphore_signal(
            barrier, inc=1, device_id={"ep": a, "tp": b, "dp": d}, device_id_type=MESH
        )
    )
    pl.semaphore_wait(barrier, nb - 1)

    def pass_block(k, block, src, a, b, d):
        pltpu.make_async_remote_copy(
            src_ref=src,
            dst_ref=xr.at[k, block],
            send_sem=xs_sem.at[k],
            recv_sem=xr_sem.at[k, block],
            device_id={"ep": a, "tp": b, "dp": d},
            device_id_type=MESH,
        ).start()

    def arrived(k, block):
        pltpu.make_async_copy(xr.at[k, block], xr.at[k, block], xr_sem.at[k, block]).wait()

    order = []
    for s in range(1, n_ep // 2 + 1):
        order.append(s)
        if n_ep - s != s:
            order.append(n_ep - s)

    def to_tp(k, block, src):
        for dx in range(1, n_tp):
            pass_block(k, block, src, z, lax.rem(x + dx, n_tp), c)

    def to_dp(k, block, src):
        for dc in range(1, n_dp):
            pass_block(k, block, src, z, x, lax.rem(c + dc, n_dp))

    for k in range(chunks):
        for s in order:
            pass_block(k, me, xin.at[k], lax.rem(z + s, n_ep), x, c)
        to_tp(k, me, xin.at[k])
        to_dp(k, me, xin.at[k])

    def ep_steps(k):
        for s in order:
            block = lax.rem(z + n_ep - s, n_ep) * nq + q
            arrived(k, block)
            to_tp(k, block, xr.at[k, block])
            to_dp(k, block, xr.at[k, block])

    def tp_steps(k):
        for s in [0] + order:
            for dx in range(1, n_tp):
                block = lax.rem(z + n_ep - s, n_ep) * nq + lax.rem(x + dx, n_tp) * n_dp + c
                arrived(k, block)
                to_dp(k, block, xr.at[k, block])

    def dp_steps(k):
        for s in [0] + order:
            for dx in range(n_tp):
                for dc in range(1, n_dp):
                    block = (
                        lax.rem(z + n_ep - s, n_ep) * nq
                        + lax.rem(x + dx, n_tp) * n_dp
                        + lax.rem(c + dc, n_dp)
                    )
                    arrived(k, block)

    def each_m(body):
        if msteps == 1:
            body(0)
        else:

            @pl.loop(0, msteps)
            def _(m):
                body(m)

    def repack(k):
        def body(m):
            part = xr[k, pl.ds(m * mb, mb), :, :depth].astype(jnp.float32)
            x2[k, pl.ds(pl.multiple_of(m * mt, mt), mt), :] = part.reshape(mt, depth).astype(
                jnp.bfloat16
            )

        each_m(body)

    def hidden_to(e, qs, b, d):
        cols = pl.ds(pl.multiple_of(qs * ff, ff), ff)
        pltpu.make_async_remote_copy(
            src_ref=hid.at[e, :, cols],
            dst_ref=hid.at[e, :, cols],
            send_sem=hs_sem.at[e],
            recv_sem=hr_sem.at[e, qs],
            device_id={"ep": z, "tp": b, "dp": d},
            device_id_type=MESH,
        ).start()

    def hidden_arrived(e, qs):
        cols = pl.ds(pl.multiple_of(qs * ff, ff), ff)
        pltpu.make_async_copy(hid.at[e, :, cols], hid.at[e, :, cols], hr_sem.at[e, qs]).wait()

    def hidden_relay(e):
        for dx in range(1, n_tp):
            qs = lax.rem(x + dx, n_tp) * n_dp + c
            hidden_arrived(e, qs)
            for dc in range(1, n_dp):
                hidden_to(e, qs, x, lax.rem(c + dc, n_dp))

    def unit(k, e):
        u = k * local + e
        s = lax.rem(u, slots)
        for copy in weights_in(u):
            copy.wait()

        def body(m):
            span = pl.ds(pl.multiple_of(m * mt, mt), mt)
            gate = jnp.dot(x2[k, span, :], gbuf[s], preferred_element_type=jnp.float32)
            up = jnp.dot(x2[k, span, :], ubuf[s], preferred_element_type=jnp.float32)
            if k > 0:
                gate = gate + acc[e, span, :ff]
                up = up + acc[e, span, ff:]
            if k < chunks - 1:
                acc[e, span, :ff] = gate
                acc[e, span, ff:] = up
            else:
                side = xr[k, pl.ds(m * mb, mb), :, depth:].astype(jnp.float32)
                side = side.reshape(mt, side.shape[2])
                lane = lax.broadcasted_iota(jnp.int32, side.shape, 1)
                named = z * local + e
                mine = (lane == named) | (lane == named + experts) | (lane == named + 2 * experts)
                weight = jnp.sum(jnp.where(mine, side, 0.0), axis=1, keepdims=True)
                hidden = gate / (1.0 + jnp.exp(-gate)) * up * weight
                cols = pl.ds(pl.multiple_of(q * ff, ff), ff)
                hid[e, span, cols] = hidden.astype(jnp.bfloat16)

        each_m(body)
        if units > slots:

            @pl.when(u + slots < units)
            def _():
                for copy in weights_in(u + slots):
                    copy.start()

            @pl.when(u == units - slots - 1)
            def _():
                for j in range(tiles):
                    down_in(j).start()

        if k == chunks - 1:
            for dx in range(1, n_tp):
                hidden_to(e, q, lax.rem(x + dx, n_tp), c)
            for dc in range(1, n_dp):
                hidden_to(e, q, x, lax.rem(c + dc, n_dp))

    ep_steps(0)
    tp_steps(0)
    own.wait()
    dp_steps(0)
    repack(0)
    for k in range(chunks):
        last = k == chunks - 1

        @pl.loop(0, local)
        def _(e):
            unit(k, e)
            if not last and local >= 4:
                pl.when(e == 0)(lambda: ep_steps(k + 1))
                pl.when(e == 2)(lambda: tp_steps(k + 1))
            if last:

                @pl.when(e >= 2)
                def _():
                    hidden_relay(e - 2)

        if not last:
            if local < 4:
                ep_steps(k + 1)
                tp_steps(k + 1)
            dp_steps(k + 1)
            repack(k + 1)

    for e in range(max(local - 2, 0), local):
        hidden_relay(e)

    @pl.loop(0, local)
    def _(e):
        for dx in range(n_tp):
            for dc in range(1, n_dp):
                hidden_arrived(e, lax.rem(x + dx, n_tp) * n_dp + lax.rem(c + dc, n_dp))

    for j in range(tiles):
        down_in(j).wait()

        def body(m):
            span = pl.ds(pl.multiple_of(m * mt, mt), mt)

            def add(e, total):
                return total + jnp.dot(
                    hid[e, span, :], dbuf[j, e], preferred_element_type=jnp.float32
                )

            total = lax.fori_loop(0, local, add, jnp.zeros((mt, tile), jnp.float32))
            pbuf[j, pl.ds(m * mb, mb)] = total.reshape(mb, rows, tile).astype(jnp.bfloat16)

        each_m(body)
        pltpu.make_async_copy(pbuf.at[j, me], back.at[j, z, q], pr_sem.at[j]).start()

        def give(a, b, d):
            pltpu.make_async_remote_copy(
                src_ref=pbuf.at[j, a * nq + b * n_dp + d],
                dst_ref=back.at[j, z, q],
                send_sem=ps_sem.at[j],
                recv_sem=pr_sem.at[j],
                device_id={"ep": a, "tp": b, "dp": d},
                device_id_type=MESH,
            ).start()

        others(give)

    for j in range(tiles):
        pltpu.make_async_copy(back.at[j], back.at[j], pr_sem.at[j]).wait()
        for qs in range(nq):
            total = back[j, 0, qs].astype(jnp.float32)
            for a in range(1, n_ep):
                total = total + back[j, a, qs].astype(jnp.float32)
            at = (qs * tiles + j) * tile
            out[:, at : at + tile] = total.astype(jnp.bfloat16)

    for k in range(chunks):
        sent = xr.at[k, pl.ds(0, nb - 1)]
        pltpu.make_async_copy(sent, sent, xs_sem.at[k]).wait()
    for e in range(local):
        sent = hid.at[e, :, pl.ds(0, (nq - 1) * ff)]
        pltpu.make_async_copy(sent, sent, hs_sem.at[e]).wait()
    for j in range(tiles):
        sent = pbuf.at[j, pl.ds(0, nb - 1)]
        pltpu.make_async_copy(sent, sent, ps_sem.at[j]).wait()


def per_device(tokens, route_weights, expert_ids, gate_weight, up_weight, down_weight):
    n_ep, n_tp, n_dp = (lax.axis_size(name) for name in ("ep", "tp", "dp"))
    nq = n_tp * n_dp
    nb = n_ep * nq
    rows, width = tokens.shape
    local, _, ff = gate_weight.shape
    _, full, part = down_weight.shape
    experts = local * n_ep
    ext = -(-3 * experts // LANES) * LANES
    chunks = CHUNKS if width % (CHUNKS * LANES) == 0 else 1
    depth = width // chunks
    slots = min(SLOTS, chunks * local)
    tile = 2 * LANES if part % (2 * LANES) == 0 else LANES
    tiles = part // tile
    count = nb * rows
    xin = routed_rows(tokens, route_weights, expert_ids, experts, chunks, ext)
    any_space = pl.BlockSpec(memory_space=pl.ANY)
    dma = pltpu.SemaphoreType.DMA
    bf16 = jnp.bfloat16
    return pl.pallas_call(
        functools.partial(kernel, (n_ep, n_tp, n_dp, experts)),
        out_shape=jax.ShapeDtypeStruct((rows, width), bf16),
        in_specs=[pl.BlockSpec(memory_space=pltpu.VMEM), any_space, any_space, any_space],
        out_specs=pl.BlockSpec(memory_space=pltpu.VMEM),
        scratch_shapes=[
            pltpu.VMEM((chunks, nb, rows, depth + ext), bf16),
            pltpu.VMEM((chunks, count, depth), bf16),
            pltpu.VMEM((slots, depth, ff), bf16),
            pltpu.VMEM((slots, depth, ff), bf16),
            pltpu.VMEM((tiles, local, full, tile), bf16),
            pltpu.VMEM((local, count, 2 * ff), jnp.float32),
            pltpu.VMEM((local, count, full), bf16),
            pltpu.VMEM((tiles, nb, rows, tile), bf16),
            pltpu.VMEM((tiles, n_ep, nq, rows, tile), bf16),
            dma((slots,)),
            dma((slots,)),
            dma((tiles,)),
            dma,
            dma((chunks,)),
            dma((chunks, nb)),
            dma((local,)),
            dma((local, nq)),
            dma((tiles,)),
            dma((tiles,)),
        ],
        compiler_params=pltpu.CompilerParams(
            collective_id=0, has_side_effects=True, vmem_limit_bytes=67043328
        ),
        name="experts",
    )(xin, gate_weight, up_weight, down_weight)


def solution(mesh):
    rows = P(("groups", "ep", "tp", "dp"), None)
    weights = P("ep", None, ("tp", "dp"))
    return jax.shard_map(
        per_device,
        mesh=mesh,
        in_specs=(rows, rows, rows, weights, weights, weights),
        out_specs=rows,
        check_vma=False,
    )
```

time: 212 us -> 59.6 us (0.28)
  waiting for transfers between devices: 87.3 us -> 0 us
  blocking collectives: 57.2 us -> 0 us
  Pallas kernels: 0 us -> 55.5 us
  matrix products: 36.6 us -> 0 us
  between operations: 13.6 us -> 0.03 us
  local copies, waits for them, and re-layouts: 9.45 us -> 2.33 us
  starting transfers between devices: 4.95 us -> 0 us
    all_to_all x2 -> x0, blocking collectives: 57.2 us -> none  [the longest x1 37.5 us: per_device(): lax.all_to_all(sendbuf, 'ep', split_axis=0, concat_axis=0, tiled=True)]
    all_gather x2 -> x0, waiting for transfers between devices: 56.5 us -> none  [the longest x1 39.5 us: per_device(): piece = lax.all_gather(arrived, ('tp', 'dp'), axis=0, tiled=True)]
    pallas_call x0 -> x1, Pallas kernels: none -> 55.5 us  [per_device(): pl.pallas_call(functools.partial(kernel, (n_ep, n_tp, n_dp, experts)), ou...]
    dot_general x3 -> x0, matrix products: 36.6 us -> none  [the longest x1 13.1 us: per_device(): jnp.einsum('gsecd,edf->gsecf', piece, gate_weight, preferred_element_type...]
    all_to_all x1 -> x0, waiting for transfers between devices: 30.9 us -> none  [per_device(): lax.all_to_all(mine, 'ep', split_axis=0, concat_axis=0, tiled=True)]
    reshape x5 -> x0, local copies, waits for them, and re-layouts: 5.16 us -> none  [the longest x2 2.39 us: per_device(): mine = mine.reshape(n_owner * exp_local, CAP, width)]
    all_to_all x1 -> x0, starting transfers between devices: 4.73 us -> none  [per_device(): lax.all_to_all(mine, 'ep', split_axis=0, concat_axis=0, tiled=True)]
    gather x3 -> x0, local copies, waits for them, and re-layouts: 2.75 us -> none  [the longest x2 1.82 us: per_device(): jnp.take(tokens, table, axis=0, mode='fill', fill_value=0)]
  transfers between devices with their start and end apart: 3 -> 0, of which waited for: 3 -> 0; matrix products, arithmetic and copies ran while one was open for 0% -> 0% of each run, Pallas kernels for 0% -> 0%
where the time goes in v1:
time: 59.6 us; the launch traced here: 59.4 us
  Pallas kernels  55.5 us (93%)
  local copies, waits for them, and re-layouts  2.33 us (4%)
  other arithmetic  1.53 us (3%)
    pallas_call x1, Pallas kernels, per_device(): pl.pallas_call(functools.partial(kernel, (n_ep, n_tp, n_dp, experts)), ou...  55.5 us
    unnamed x1, local copies, waits for them, and re-layouts  1.53 us

profile of v1, /device:TPU:0, one launch (start us, length us, event | category | flops | bytes accessed | tf_op | source)
XLA Modules:
  0.0 59.4 jit_solution(4312976692335471057)
XLA Ops:
  0.0 0.8 %select_reduce_fusion = f32[8,32]{1,0:T(8,128)S(1)} fusion(f32[8,8]{1,0:T(8,128)} %param.7, s32[8,8]{1,0:T(8,128)} %param.8), kind=kLoop, calls=%fused_computation.5 | loop fusion | flops 5888 | bytes 1536 | tf_op jit(solution)/shard_map/reduce_sum | solution.py:18
  0.8 0.1 fusion.7
  0.9 0.8 %fusion.8 = (bf16[8,2560]{1,0:T(8,128)(2,1)S(1)}, bf16[8,2560]{1,0:T(8,128)(2,1)S(1)}) fusion(bf16[8,5120]{1,0:T(8,128)(2,1)} %param.6), kind=kLoop, calls=%fused_computation.18 | loop fusion | bytes 163840 | tf_op jit(solution)/shard_map/slice | solution.py:30
  1.7 0.7 %pad_maximum_fusion.xin = bf16[2,8,2688]{2,1,0:T(8,128)(2,1)} fusion(bf16[1,8,2688]{2,1,0:T(8,128)(2,1)S(1)} %get-tuple-element.11, bf16[1,8,2688]{2,1,0:T(8,128)(2,1)S(1)} %get-tuple-element.10), kind=kLoop, calls=%fused_computation | loop fusion | flops 43008 | bytes 172032 | tf_op jit(solution)/shard_map/stack | solution.py:28
  2.4 55.5 %experts.1 = bf16[8,5120]{1,0:T(8,128)(2,1)} custom-call(bf16[2,8,2688]{2,1,0:T(8,128)(2,1)} %pad_maximum_fusion.xin, bf16[8,5120,256]{2,1,0:T(8,128)(2,1)} %gate_hbm.1, bf16[8,5120,256]{2,1,0:T(8,128)(2,1)} %up_hbm.1, bf16[8,1024,1280]{2,1,0:T(8,128)(2,1)} %down_hbm.1), custom_call_target="tpu_custom_call" | custom-call | tf_op jit(solution)/shard_map/experts/pallas_call | solution.py:368
  57.8 1.5 %copy.8 = bf16[8,5120]{1,0:T(8,128)(2,1)} copy(bf16[8,5120]{1,0:T(8,128)(2,1)} %experts.1) | data formatting | bytes 163840
  (2 shorter events, 0.0 us)

commit v2 on v1

--- a/solution.py
+++ b/solution.py
@@ -9,44 +9,47 @@
 
 MESH = pl.DeviceIdType.MESH
 LANES = 128
-CHUNKS = 2
-SLOTS = 12
-
-
-def routed_rows(tokens, route_weights, expert_ids, experts, chunks, ext):
-    lane = jnp.arange(experts, dtype=jnp.int32)
-    dense = jnp.sum(
-        jnp.where(expert_ids[:, :, None] == lane, route_weights[:, :, None], 0.0), axis=1
-    )
-    first = lax.reduce_precision(dense, 8, 7)
-    second = lax.reduce_precision(dense - first, 8, 7)
-    third = dense - first - second
-    side = jnp.concatenate([first, second, third], axis=1).astype(jnp.bfloat16)
-    side = jnp.pad(side, ((0, 0), (0, ext - side.shape[1])))
-    rows, width = tokens.shape
-    depth = width // chunks
-    return jnp.stack(
-        [
-            jnp.concatenate([tokens[:, k * depth : (k + 1) * depth], side], axis=1)
-            for k in range(chunks)
-        ]
-    )
+CHUNKS = 4
+SLOTS = 24
+CAP = 4
+
+
+def rows_and_routes(tokens, route_weights, expert_ids, xin, experts):
+    chunks, rows, wide = xin.shape
+    depth = tokens.shape[1] // chunks
+    weight, ids = route_weights[...], expert_ids[...]
+    lane = lax.broadcasted_iota(jnp.int32, (rows, wide - depth), 1)
+    side = jnp.zeros((rows, wide - depth), jnp.float32)
+    for term in range(3):
+        held = weight.astype(jnp.bfloat16).astype(jnp.float32)
+        weight = weight - held
+        for k in range(ids.shape[1]):
+            hit = lane == ids[:, k : k + 1] + term * experts
+            side = side + jnp.where(hit, held[:, k : k + 1], 0.0)
+    for k in range(chunks):
+        xin[k, :, :depth] = tokens[:, k * depth : (k + 1) * depth]
+        xin[k, :, depth:] = side.astype(jnp.bfloat16)
 
 
 def kernel(
     dims,
-    xin,
+    tokens,
+    route_weights,
+    expert_ids,
     gate_hbm,
     up_hbm,
     down_hbm,
     out,
+    xin,
     xr,
     x2,
     gbuf,
     ubuf,
     dbuf,
     acc,
+    packed,
     hid,
+    ranks,
     pbuf,
     back,
     g_sem,
@@ -70,16 +73,20 @@
     ff = gbuf.shape[2]
     tiles, _, full, tile = dbuf.shape
     units = chunks * local
+    groups = 2 if local % 4 == 0 else 1
+    ge = local // groups
+    packed_rows = packed.shape[1]
     mt = min(count, 128)
     mb = mt // rows
     msteps = count // mt
+    ms = packed_rows // msteps
 
     z, x, c = lax.axis_index("ep"), lax.axis_index("tp"), lax.axis_index("dp")
     q = x * n_dp + c
     me = z * nq + q
 
     def weights_in(u):
-        k, e = u // local, u % local
+        k, e = u % (chunks * ge) // ge, u // (chunks * ge) * ge + u % ge
         s = u % slots
         span = pl.ds(pl.multiple_of(k * depth, depth), depth)
         return (
@@ -98,6 +105,7 @@
     if units <= slots:
         for j in range(tiles):
             down_in(j).start()
+    rows_and_routes(tokens, route_weights, expert_ids, xin, experts)
     own = pltpu.make_async_copy(xin, xr.at[:, me], own_sem)
     own.start()
 
@@ -193,11 +201,41 @@
 
         each_m(body)
 
+    def routes(k, m):
+        side = xr[k, pl.ds(m * mb, mb), :, depth:].astype(jnp.float32)
+        return side.reshape(mt, side.shape[2])
+
+    def rank_rows(k):
+        def body(m):
+            named = (routes(k, m) > 0.0).astype(jnp.float32)
+            row = lax.broadcasted_iota(jnp.int32, (mt, mt), 0)
+            col = lax.broadcasted_iota(jnp.int32, (mt, mt), 1)
+            before = (row // rows == col // rows) & (col < row)
+            count_before = jnp.dot(
+                before.astype(jnp.float32).astype(jnp.bfloat16),
+                named.astype(jnp.bfloat16),
+                preferred_element_type=jnp.float32,
+            )
+            ranks[pl.ds(pl.multiple_of(m * mt, mt), mt), :] = jnp.where(
+                named > 0.0, count_before, -1.0
+            )
+
+        each_m(body)
+
+    def places(e, span):
+        table = ranks[span, :]
+        lane = lax.broadcasted_iota(jnp.int32, table.shape, 1)
+        rank = jnp.sum(jnp.where(lane == z * local + e, table, 0.0), axis=1, keepdims=True)
+        row = lax.broadcasted_iota(jnp.int32, (mt, ms), 0)
+        slot = lax.broadcasted_iota(jnp.int32, (mt, ms), 1)
+        mine = (row // rows == slot // CAP) & ((slot % CAP).astype(jnp.float32) == rank)
+        return mine.astype(jnp.float32).astype(jnp.bfloat16)
+
     def hidden_to(e, qs, b, d):
         cols = pl.ds(pl.multiple_of(qs * ff, ff), ff)
         pltpu.make_async_remote_copy(
-            src_ref=hid.at[e, :, cols],
-            dst_ref=hid.at[e, :, cols],
+            src_ref=packed.at[e, :, cols],
+            dst_ref=packed.at[e, :, cols],
             send_sem=hs_sem.at[e],
             recv_sem=hr_sem.at[e, qs],
             device_id={"ep": z, "tp": b, "dp": d},
@@ -206,7 +244,7 @@
 
     def hidden_arrived(e, qs):
         cols = pl.ds(pl.multiple_of(qs * ff, ff), ff)
-        pltpu.make_async_copy(hid.at[e, :, cols], hid.at[e, :, cols], hr_sem.at[e, qs]).wait()
+        pltpu.make_async_copy(packed.at[e, :, cols], packed.at[e, :, cols], hr_sem.at[e, qs]).wait()
 
     def hidden_relay(e):
         for dx in range(1, n_tp):
@@ -216,7 +254,7 @@
                 hidden_to(e, qs, x, lax.rem(c + dc, n_dp))
 
     def unit(k, e):
-        u = k * local + e
+        u = e // ge * (chunks * ge) + k * ge + e % ge
         s = lax.rem(u, slots)
         for copy in weights_in(u):
             copy.wait()
@@ -232,15 +270,21 @@
                 acc[e, span, :ff] = gate
                 acc[e, span, ff:] = up
             else:
-                side = xr[k, pl.ds(m * mb, mb), :, depth:].astype(jnp.float32)
-                side = side.reshape(mt, side.shape[2])
+                side = routes(k, m)
+                named = z * local + e
                 lane = lax.broadcasted_iota(jnp.int32, side.shape, 1)
-                named = z * local + e
                 mine = (lane == named) | (lane == named + experts) | (lane == named + 2 * experts)
                 weight = jnp.sum(jnp.where(mine, side, 0.0), axis=1, keepdims=True)
                 hidden = gate / (1.0 + jnp.exp(-gate)) * up * weight
+                kept = lax.dot_general(
+                    places(e, span),
+                    hidden.astype(jnp.bfloat16),
+                    (((0,), (0,)), ((), ())),
+                    preferred_element_type=jnp.float32,
+                )
                 cols = pl.ds(pl.multiple_of(q * ff, ff), ff)
-                hid[e, span, cols] = hidden.astype(jnp.bfloat16)
+                slot = pl.ds(pl.multiple_of(m * ms, ms), ms)
+                packed[e, slot, cols] = kept.astype(jnp.bfloat16)
 
         each_m(body)
         if units > slots:
@@ -266,27 +310,29 @@
     own.wait()
     dp_steps(0)
     repack(0)
-    for k in range(chunks):
-        last = k == chunks - 1
-
-        @pl.loop(0, local)
-        def _(e):
-            unit(k, e)
-            if not last and local >= 4:
-                pl.when(e == 0)(lambda: ep_steps(k + 1))
-                pl.when(e == 2)(lambda: tp_steps(k + 1))
-            if last:
-
-                @pl.when(e >= 2)
-                def _():
-                    hidden_relay(e - 2)
-
-        if not last:
-            if local < 4:
-                ep_steps(k + 1)
-                tp_steps(k + 1)
-            dp_steps(k + 1)
-            repack(k + 1)
+    rank_rows(0)
+    for g in range(groups):
+        for k in range(chunks):
+            last = k == chunks - 1
+            ahead = g == 0 and not last
+
+            @pl.loop(0, ge)
+            def _(i):
+                unit(k, g * ge + i)
+                if ahead and ge >= 4:
+                    pl.when(i == 0)(lambda: ep_steps(k + 1))
+                    pl.when(i == 2)(lambda: tp_steps(k + 1))
+                if g > 0 and k == 0:
+                    pl.when(i < 2)(lambda: hidden_relay(g * ge - 2 + i))
+                if last and ge >= 2:
+                    pl.when(i >= 2)(lambda: hidden_relay(g * ge + i - 2))
+
+            if ahead:
+                if ge < 4:
+                    ep_steps(k + 1)
+                    tp_steps(k + 1)
+                dp_steps(k + 1)
+                repack(k + 1)
 
     for e in range(max(local - 2, 0), local):
         hidden_relay(e)
@@ -296,6 +342,16 @@
         for dx in range(n_tp):
             for dc in range(1, n_dp):
                 hidden_arrived(e, lax.rem(x + dx, n_tp) * n_dp + lax.rem(c + dc, n_dp))
+
+        def body(m):
+            span = pl.ds(pl.multiple_of(m * mt, mt), mt)
+            slot = pl.ds(pl.multiple_of(m * ms, ms), ms)
+            spread = jnp.dot(
+                places(e, span), packed[e, slot, :], preferred_element_type=jnp.float32
+            )
+            hid[e, span, :] = spread.astype(jnp.bfloat16)
+
+        each_m(body)
 
     for j in range(tiles):
         down_in(j).wait()
@@ -339,7 +395,7 @@
         sent = xr.at[k, pl.ds(0, nb - 1)]
         pltpu.make_async_copy(sent, sent, xs_sem.at[k]).wait()
     for e in range(local):
-        sent = hid.at[e, :, pl.ds(0, (nq - 1) * ff)]
+        sent = packed.at[e, :, pl.ds(0, (nq - 1) * ff)]
         pltpu.make_async_copy(sent, sent, hs_sem.at[e]).wait()
     for j in range(tiles):
         sent = pbuf.at[j, pl.ds(0, nb - 1)]
@@ -361,23 +417,26 @@
     tile = 2 * LANES if part % (2 * LANES) == 0 else LANES
     tiles = part // tile
     count = nb * rows
-    xin = routed_rows(tokens, route_weights, expert_ids, experts, chunks, ext)
+    in_vmem = pl.BlockSpec(memory_space=pltpu.VMEM)
     any_space = pl.BlockSpec(memory_space=pl.ANY)
     dma = pltpu.SemaphoreType.DMA
     bf16 = jnp.bfloat16
     return pl.pallas_call(
         functools.partial(kernel, (n_ep, n_tp, n_dp, experts)),
         out_shape=jax.ShapeDtypeStruct((rows, width), bf16),
-        in_specs=[pl.BlockSpec(memory_space=pltpu.VMEM), any_space, any_space, any_space],
-        out_specs=pl.BlockSpec(memory_space=pltpu.VMEM),
+        in_specs=[in_vmem] * 3 + [any_space] * 3,
+        out_specs=in_vmem,
         scratch_shapes=[
+            pltpu.VMEM((chunks, rows, depth + ext), bf16),
             pltpu.VMEM((chunks, nb, rows, depth + ext), bf16),
             pltpu.VMEM((chunks, count, depth), bf16),
             pltpu.VMEM((slots, depth, ff), bf16),
             pltpu.VMEM((slots, depth, ff), bf16),
             pltpu.VMEM((tiles, local, full, tile), bf16),
             pltpu.VMEM((local, count, 2 * ff), jnp.float32),
+            pltpu.VMEM((local, nb * CAP, full), bf16),
             pltpu.VMEM((local, count, full), bf16),
+            pltpu.VMEM((count, ext), jnp.float32),
             pltpu.VMEM((tiles, nb, rows, tile), bf16),
             pltpu.VMEM((tiles, n_ep, nq, rows, tile), bf16),
             dma((slots,)),
@@ -395,7 +454,7 @@
             collective_id=0, has_side_effects=True, vmem_limit_bytes=67043328
         ),
         name="experts",
-    )(xin, gate_weight, up_weight, down_weight)
+    )(tokens, route_weights, expert_ids, gate_weight, up_weight, down_weight)
 
 
 def solution(mesh):

time: 59.6 us -> 66.6 us (1.12)
  Pallas kernels: 55.5 us -> 64.9 us
  other arithmetic: 1.53 us -> 0 us
  local copies, waits for them, and re-layouts: 2.33 us -> 1.53 us
    pallas_call x1, Pallas kernels: 55.5 us -> 64.9 us  [per_device(): pl.pallas_call(functools.partial(kernel, (n_ep, n_tp, n_dp, experts)), ou...]
    slice x1 -> x0, local copies, waits for them, and re-layouts: 0.81 us -> none  [routed_rows(): tokens[:, k * depth:(k + 1) * depth]]
    reduce_sum x1 -> x0, other arithmetic: 0.79 us -> none  [routed_rows(): jnp.sum(jnp.where(expert_ids[:, :, None] == lane, route_weights[:, :, Non...]
where the time goes in v2:
time: 66.6 us; the launch traced here: 66.4 us
  Pallas kernels  64.9 us (97%)
  local copies, waits for them, and re-layouts  1.53 us (2%)
    pallas_call x1, Pallas kernels, per_device(): pl.pallas_call(functools.partial(kernel, (n_ep, n_tp, n_dp, experts)), ou...  64.9 us
    unnamed x1, local copies, waits for them, and re-layouts  1.53 us

profile of v2, /device:TPU:0, one launch (start us, length us, event | category | flops | bytes accessed | tf_op | source)
XLA Modules:
  0.0 66.4 jit_solution(5389690389881863056)
XLA Ops:
  0.0 64.9 %experts.1 = bf16[8,5120]{1,0:T(8,128)(2,1)} custom-call(bf16[8,5120]{1,0:T(8,128)(2,1)} %tokens.1, f32[8,8]{1,0:T(8,128)} %route_weights.1, s32[8,8]{1,0:T(8,128)} %expert_ids.1, bf16[8,5120,256]{2,1,0:T(8,128)(2,1)} %gate_hbm.1, bf16[8,5120,256]{2,1,0:T(8,128)(2,1)} %up_hbm.1, bf16[8,1024,1280]{2,1,0:T(8,128)(2,1)} %down_hbm.1), custom_call_target="tpu_custom_call" | custom-call | tf_op jit(solution)/shard_map/experts/pallas_call | solution.py:424
  64.9 1.5 %copy.8 = bf16[8,5120]{1,0:T(8,128)(2,1)} copy(bf16[8,5120]{1,0:T(8,128)(2,1)} %experts.1) | data formatting | bytes 163840

commit v3 on v2

--- a/solution.py
+++ b/solution.py
@@ -9,8 +9,8 @@
 
 MESH = pl.DeviceIdType.MESH
 LANES = 128
-CHUNKS = 4
-SLOTS = 24
+CHUNKS = 1
+SLOTS = 6
 CAP = 4
 
 
@@ -50,6 +50,7 @@
     packed,
     hid,
     ranks,
+    offsets,
     pbuf,
     back,
     g_sem,
@@ -206,18 +207,23 @@
         return side.reshape(mt, side.shape[2])
 
     def rank_rows(k):
+        row = lax.broadcasted_iota(jnp.int32, (mt, ms), 0)
+        slot = lax.broadcasted_iota(jnp.int32, (mt, ms), 1)
+        offset = slot - lax.div(row, rows) * CAP
+        offsets[...] = offset.astype(jnp.float32)
+
         def body(m):
             named = (routes(k, m) > 0.0).astype(jnp.float32)
             row = lax.broadcasted_iota(jnp.int32, (mt, mt), 0)
             col = lax.broadcasted_iota(jnp.int32, (mt, mt), 1)
-            before = (row // rows == col // rows) & (col < row)
+            before = (col < row) & (col >= row - lax.rem(row, rows))
             count_before = jnp.dot(
                 before.astype(jnp.float32).astype(jnp.bfloat16),
                 named.astype(jnp.bfloat16),
                 preferred_element_type=jnp.float32,
             )
             ranks[pl.ds(pl.multiple_of(m * mt, mt), mt), :] = jnp.where(
-                named > 0.0, count_before, -1.0
+                named > 0.0, count_before, -float(packed_rows)
             )
 
         each_m(body)
@@ -226,10 +232,7 @@
         table = ranks[span, :]
         lane = lax.broadcasted_iota(jnp.int32, table.shape, 1)
         rank = jnp.sum(jnp.where(lane == z * local + e, table, 0.0), axis=1, keepdims=True)
-        row = lax.broadcasted_iota(jnp.int32, (mt, ms), 0)
-        slot = lax.broadcasted_iota(jnp.int32, (mt, ms), 1)
-        mine = (row // rows == slot // CAP) & ((slot % CAP).astype(jnp.float32) == rank)
-        return mine.astype(jnp.float32).astype(jnp.bfloat16)
+        return jnp.where(offsets[...] == rank, 1.0, 0.0).astype(jnp.bfloat16)
 
     def hidden_to(e, qs, b, d):
         cols = pl.ds(pl.multiple_of(qs * ff, ff), ff)
@@ -364,7 +367,7 @@
                     hid[e, span, :], dbuf[j, e], preferred_element_type=jnp.float32
                 )
 
-            total = lax.fori_loop(0, local, add, jnp.zeros((mt, tile), jnp.float32))
+            total = lax.fori_loop(0, local, add, jnp.zeros((mt, tile), jnp.float32), unroll=True)
             pbuf[j, pl.ds(m * mb, mb)] = total.reshape(mb, rows, tile).astype(jnp.bfloat16)
 
         each_m(body)
@@ -437,6 +440,7 @@
             pltpu.VMEM((local, nb * CAP, full), bf16),
             pltpu.VMEM((local, count, full), bf16),
             pltpu.VMEM((count, ext), jnp.float32),
+            pltpu.VMEM((min(count, 128), min(count, 128) // rows * CAP), jnp.float32),
             pltpu.VMEM((tiles, nb, rows, tile), bf16),
             pltpu.VMEM((tiles, n_ep, nq, rows, tile), bf16),
             dma((slots,)),

time: 66.6 us -> 50.3 us (0.76)
  Pallas kernels: 64.9 us -> 48.6 us
    pallas_call x1, Pallas kernels: 64.9 us -> 48.6 us  [per_device(): pl.pallas_call(functools.partial(kernel, (n_ep, n_tp, n_dp, experts)), ou...]
where the time goes in v3:
time: 50.3 us; the launch traced here: 50.1 us
  Pallas kernels  48.6 us (97%)
  local copies, waits for them, and re-layouts  1.53 us (3%)
    pallas_call x1, Pallas kernels, per_device(): pl.pallas_call(functools.partial(kernel, (n_ep, n_tp, n_dp, experts)), ou...  48.6 us
    unnamed x1, local copies, waits for them, and re-layouts  1.53 us

profile of v3, /device:TPU:0, one launch (start us, length us, event | category | flops | bytes accessed | tf_op | source)
XLA Modules:
  0.0 50.1 jit_solution(4082622053844088944)
XLA Ops:
  0.0 48.6 %experts.1 = bf16[8,5120]{1,0:T(8,128)(2,1)} custom-call(bf16[8,5120]{1,0:T(8,128)(2,1)} %tokens.1, f32[8,8]{1,0:T(8,128)} %route_weights.1, s32[8,8]{1,0:T(8,128)} %expert_ids.1, bf16[8,5120,256]{2,1,0:T(8,128)(2,1)} %gate_hbm.1, bf16[8,5120,256]{2,1,0:T(8,128)(2,1)} %up_hbm.1, bf16[8,1024,1280]{2,1,0:T(8,128)(2,1)} %down_hbm.1), custom_call_target="tpu_custom_call" | custom-call | tf_op jit(solution)/shard_map/experts/pallas_call | solution.py:427
  48.6 1.5 %copy.8 = bf16[8,5120]{1,0:T(8,128)(2,1)} copy(bf16[8,5120]{1,0:T(8,128)(2,1)} %experts.1) | data formatting | bytes 163840
